TPU v7x, 32 devices: a whole 2x2x4 slice. The times are simulated.
32 devices in a mesh: groups: 2 (over y), range: 8 (over z, x), sub: 2 (over core).
Axes of the slice: x: 2, y: 2, z: 4, core: 2. Of those that a mesh axis runs over, the one named last changes fastest.
Arguments:
- samples: float32 [2, 1024, 32, 128], P(None, ('groups', 'range', 'sub')), parts along dimension 1, may hold values from -6 to 6
- beam_weights: float32 [32, 8, 2, 64, 128], P(('groups', 'range'), None, None, None, 'sub'), parts along dimension 0, may hold values from -0.25 to 0.25
- subarrays: int32 [32, 8, 64], P(('groups', 'range', 'sub')), parts along dimension 0, may hold values from 0 to 511, as said below
- training: int32 [64], P(('groups', 'range', 'sub')), parts along dimension 0, may hold values 0 or 1
Outputs:
- covariance: float32 [32, 8, 64, 128], P(('groups', 'range', 'sub')), parts along dimension 0
- filtered: float32 [2, 128, 64, 128], P(None, None, ('groups', 'range', 'sub')), parts along dimension 2
- energy: float32 [256], P('groups'), parts along dimension 0
There are 2 independent parts, one for each index of `groups`. A program takes and returns all parts, laid end to end along the dimension named above; each array names one. Nothing has to cross between parts.
Inputs may be any that keep to these rules, and one draw needn't show every extreme that they name: `subarrays`: in each gate block the 512 indices are all 512 channels, each once.
All inputs are finite; a program needn't handle non-finite values. No bound on the sum of `training` on one device may be relied on, other than what follows from the above.
Results may differ from a plain program's by a relative error of at most 0.0003.
Values sent between devices are 32-bit elements; how exact they have to be, the bound alone decides.
A program may use at most 64 MiB of HBM per device.

v0:
```python
import jax
import jax.numpy as jnp
from jax import lax
from jax.sharding import PartitionSpec as P

GB = 2
loading = 0.05


def block_terms(snaps, chosen, weights, masked, factor):
    highest = lax.Precision.HIGHEST
    picked = jnp.take(snaps, chosen, axis=1)
    real_part = picked[0]
    imag_part = picked[1]
    real_masked = real_part * masked
    imag_masked = imag_part * masked
    cov_real = (
        jnp.einsum("snx,smx->snm", real_masked, real_part, precision=highest)
        + jnp.einsum("snx,smx->snm", imag_masked, imag_part, precision=highest)
    ) * factor
    cov_imag = (
        jnp.einsum("snx,smx->snm", imag_masked, real_part, precision=highest)
        - jnp.einsum("snx,smx->snm", real_masked, imag_part, precision=highest)
    ) * factor
    w_real = weights[:, 0]
    w_imag = weights[:, 1]
    out_real = jnp.einsum("snk,snx->kx", w_real, real_part, precision=highest) + jnp.einsum(
        "snk,snx->kx", w_imag, imag_part, precision=highest
    )
    out_imag = jnp.einsum("snk,snx->kx", w_real, imag_part, precision=highest) - jnp.einsum(
        "snk,snx->kx", w_imag, real_part, precision=highest
    )
    prod_real = jnp.einsum("snm,smk->snk", cov_real, w_real, precision=highest) - jnp.einsum(
        "snm,smk->snk", cov_imag, w_imag, precision=highest
    )
    prod_imag = jnp.einsum("snm,smk->snk", cov_real, w_imag, precision=highest) + jnp.einsum(
        "snm,smk->snk", cov_imag, w_real, precision=highest
    )
    quadratic = jnp.sum(w_real * prod_real + w_imag * prod_imag, axis=(0, 1))
    inverse = 1.0 / jnp.sqrt(quadratic + loading)
    filtered = jnp.stack([out_real * inverse[:, None], out_imag * inverse[:, None]])
    energy = jnp.sum(out_real * out_real + out_imag * out_imag, axis=1)
    covariance = jnp.concatenate([cov_real, cov_imag], axis=-1)
    return (covariance, filtered, energy)


def body(samples, beam_weights, subarrays, training):
    range_count = lax.axis_size("range")
    core_count = lax.axis_size("sub")
    parts_iq, chan_dev, all_gates, pulses = samples.shape
    gate_dev = all_gates // (range_count * core_count)
    channels = chan_dev * range_count * core_count
    blocks_dev = gate_dev // GB
    spread = samples.reshape(parts_iq, 1, 1, chan_dev, range_count, core_count, gate_dev, pulses)
    turned = lax.all_to_all(
        lax.all_to_all(spread, "range", split_axis=4, concat_axis=1, tiled=True),
        "sub",
        split_axis=5,
        concat_axis=2,
        tiled=True,
    )
    local_data = turned.reshape(parts_iq, channels, blocks_dev, GB * pulses).transpose(2, 0, 1, 3)
    mine = lax.all_to_all(beam_weights, "sub", split_axis=0, concat_axis=4, tiled=True)
    gates_on = training.astype(jnp.float32).reshape(blocks_dev, GB)
    masked = jnp.repeat(gates_on, pulses, axis=1)
    factor = 1.0 / (GB * pulses)
    covs, filts, energies = jax.vmap(block_terms, in_axes=(0, 0, 0, 0, None))(
        local_data, subarrays, mine, masked, factor
    )
    beams = filts.shape[2]
    filtered = filts.reshape(blocks_dev, parts_iq, beams, GB, pulses).transpose(1, 2, 0, 3, 4)
    filtered = filtered.reshape(parts_iq, beams, gate_dev, pulses)
    total = lax.psum(jnp.sum(energies, axis=0), ("range", "sub"))
    energy = total / (all_gates * pulses)
    return (covs, filtered, energy)


def solution(mesh):
    placed = (
        P(None, ("groups", "range", "sub"), None, None),
        P(("groups", "range"), None, None, None, "sub"),
        P(("groups", "range", "sub"), None, None),
        P(("groups", "range", "sub")),
    )
    return jax.shard_map(
        body,
        mesh=mesh,
        in_specs=placed,
        out_specs=(
            P(("groups", "range", "sub"), None, None, None),
            P(None, None, ("groups", "range", "sub"), None),
            P("groups"),
        ),
        check_vma=False,
    )
```

profile of v0, /device:TPU:0, one launch (start us, length us, event | category | flops | bytes accessed | tf_op | source)
XLA Modules:
  0.0 92.5 jit_solution(9004139148378862796)
XLA Ops:
  0.6 2.5 %reshape.157 = f32[2,1,65536]{2,1,0:T(1,128)} reshape(f32[2,8,2,64,64]{4,3,2,1,0:T(8,128)} %param.5) | data formatting | bytes 1048576
  3.2 3.5 %all-to-all-start.2 = ((f32[2,1,65536]{2,1,0:T(1,128)}), f32[2,1,65536]{2,1,0:T(1,128)S(1)}, u32[]{:S(2)}, u32[]{:S(2)}) async-start(f32[2,1,65536]{2,1,0:T(1,128)} %reshape.157), calls=%async_computation.2 | async-start | bytes 1048576 | tf_op jit(solution)/shard_map/all_to_all | solution.py:63
  6.7 1.6 %copy.24 = f32[2,1,1,32,8,2,2,128]{7,6,3,5,0,2,1,4:T(2,128)} copy(f32[2,1,1,32,8,2,2,128]{7,6,5,4,3,0,2,1:T(2,128)S(1)} %bitcast.103) | data formatting | bytes 2097152 | tf_op jit(solution)/shard_map/reshape | solution.py:54
  8.2 0.2 all-to-all-done.2
  8.4 7.4 %all-to-all-start = ((f32[2,1,1,32,8,2,2,128]{7,6,3,5,0,2,1,4:T(2,128)}), f32[2,1,1,32,8,2,2,128]{7,6,3,5,0,2,1,4:T(2,128)S(1)}, u32[]{:S(2)}, u32[]{:S(2)}) async-start(f32[2,1,1,32,8,2,2,128]{7,6,3,5,0,2,1,4:T(2,128)} %copy.24), calls=%async_computation | async-start | bytes 2097152 | tf_op jit(solution)/shard_map/all_to_all | solution.py:56
  15.9 0.5 broadcast.75
  16.4 2.3 %reduce.5 = f32[2,65536]{1,0:T(2,128)S(1)} reduce(f32[2,1,65536]{2,1,0:T(1,128)S(1)} %all-to-all-done.2, f32[]{:T(128)} %broadcast.75), dimensions={1}, to_apply=%all_to_all.44.reduce_sub_computation | reduce | bytes 1048580 | tf_op jit(solution)/shard_map/all_to_all | solution.py:63
  18.8 0.6 reshape.158
  19.4 1.9 %copy.29 = f32[1,8,2,64,2,64]{5,4,3,1,2,0:T(2,128)} copy(f32[1,8,2,64,2,64]{5,3,2,1,4,0:T(8,128)S(1)} %bitcast.98) | data formatting | bytes 1048576 | tf_op jit(solution)/shard_map/all_to_all | solution.py:63
  21.2 1.8 %all_to_all.47 = f32[1,8,2,64,128]{4,3,1,2,0:T(8,128)S(1)} reshape(f32[1,8,2,64,2,64]{5,4,3,1,2,0:T(2,128)} %copy.29) | data formatting | bytes 1048576 | tf_op jit(solution)/shard_map/all_to_all | solution.py:63
  23.1 18.9 %all-to-all-done = f32[2,1,1,32,8,2,2,128]{7,6,3,5,0,2,1,4:T(2,128)S(1)} async-done(((f32[2,1,1,32,8,2,2,128]{7,6,3,5,0,2,1,4:T(2,128)}), f32[2,1,1,32,8,2,2,128]{7,6,3,5,0,2,1,4:T(2,128)S(1)}, u32[]{:S(2)}, u32[]{:S(2)}) %all-to-all-start) | async-done | bytes 1048608 | tf_op jit(solution)/shard_map/all_to_all | solution.py:56
  42.1 4.6 %all_to_all.51 = f32[2,8,1,32,1,2,2,128]{7,6,3,1,0,4,2,5:T(2,128)S(1)} all-to-all(f32[2,8,1,32,1,2,2,128]{7,6,3,1,0,4,2,5:T(2,128)S(1)} %copy.25), channel_id=1, replica_groups=mesh['groups'=2,'range'=8,'sub'=2] {'sub'}, dimensions={5} | all-to-all | bytes 2097152 | tf_op jit(solution)/shard_map/all_to_all | solution.py:55
  46.8 0.8 copy.27
  47.6 2.3 %gather_fusion = f32[512,2,256]{2,1,0:T(2,128)S(1)} fusion(f32[1,2,512,256]{3,1,2,0:T(2,128)S(1)} %copy.27, s32[512]{0:T(512)S(1)} %reshape.147), kind=kCustom, calls=%fused_computation | custom fusion | bytes 2101248 | tf_op jit(solution)/shard_map/vmap(jit(_take))/gather | solution.py:12
  50.1 0.1 broadcast_select_fusion
  50.2 1.0 %convolution_bitcast_fusion.2 = f32[256,128]{1,0:T(8,128)S(1)} fusion(f32[1,2,8,64,256]{4,3,2,1,0:T(8,128)S(1)} %broadcast_select_fusion, f32[1,8,2,64,128]{4,3,1,2,0:T(8,128)S(1)} %all_to_all.47), kind=kOutput, calls=%fused_computation.13 | convolution fusion | flops 201326592 | bytes 917504 | tf_op jit(solution)/shard_map/vmap(snk,snx->kx)/dot_general | solution.py:27
  51.2 1.0 %convolution_bitcast_fusion = f32[256,128]{1,0:T(8,128)S(1)} fusion(f32[1,2,8,64,256]{4,3,2,1,0:T(8,128)S(1)} %broadcast_select_fusion, f32[1,8,2,64,128]{4,3,1,2,0:T(8,128)S(1)} %all_to_all.47), kind=kOutput, calls=%fused_computation.11 | convolution fusion | flops 201326592 | bytes 917504 | tf_op jit(solution)/shard_map/vmap(snk,snx->kx)/dot_general | solution.py:30
  52.2 0.6 fusion.12
  52.9 0.6 fusion.2
  53.5 0.4 fusion.19
  53.9 0.4 fusion.18
  54.3 0.6 fusion.8
  54.9 1.0 %fusion.6 = f32[256,128]{1,0:T(8,128)S(1)} fusion(f32[256,128]{1,0:T(8,128)S(1)} %convolution_bitcast_fusion.2, f32[1,2,8,64,256]{4,3,2,1,0:T(8,128)S(1)} %broadcast_select_fusion, f32[1,8,2,64,128]{4,3,1,2,0:T(8,128)S(1)} %all_to_all.47), kind=kOutput, calls=%fused_computation.15 | convolution fusion | flops 201359360 | bytes 1048576 | tf_op jit(solution)/shard_map/vmap(snk,snx->kx)/dot_general | solution.py:27
  55.9 0.6 fusion.3
  56.5 0.4 fusion
  56.9 0.4 fusion.5
  57.4 1.0 %add_reduce_fusion = (f32[128]{0:T(128)S(1)}, f32[256,128]{1,0:T(8,128)S(1)}, f32[256,128]{1,0:T(8,128)S(1)}) fusion(f32[256,128]{1,0:T(8,128)S(1)} %fusion.6, f32[128]{0:T(128)S(1)} %add_rsqrt_fusion, f32[256,128]{1,0:T(8,128)S(1)} %convolution_bitcast_fusion, f32[1,8,2,64,128]{4,3,1,2,0:T(8,128)S(1)} %all_to_all.47, ...), kind=kOutput, calls=%fused_computation.36 | convolution fusion | flops 201555840 | bytes 1311744 | tf_op jit(solution)/shard_map/vmap(snk,snx->kx)/dot_general | solution.py:30
  58.4 31.6 %psum.7 = f32[128]{0:T(128)S(1)} all-reduce(f32[128]{0:T(128)S(1)} %get-tuple-element.3), channel_id=1, replica_groups=mesh['groups'=2,'range'=8,'sub'=2] {'range','sub'}, use_global_device_ids=true, to_apply=%region_2.3 | all-reduce | flops 128 | bytes 1024 | tf_op jit(solution)/shard_map/psum | solution.py:73
  90.1 0.5 broadcast_multiply_fusion.2
  90.7 0.1 copy.31
  90.8 0.8 pad_maximum_fusion
  91.7 0.8 pad_maximum_fusion.1
  (18 shorter events, 0.5 us)
Async XLA Ops:
  0.6 6.0 %copy-start = (f32[2,32,32,128]{3,2,1,0:T(8,128)S(1)}, f32[2,32,32,128]{3,2,1,0:T(8,128)}, u32[]{:S(2)}) copy-start(f32[2,32,32,128]{3,2,1,0:T(8,128)} %param.4) | copy-start | bytes 3145732
  3.2 5.2 %all-to-all-start.2 = ((f32[2,1,65536]{2,1,0:T(1,128)}), f32[2,1,65536]{2,1,0:T(1,128)S(1)}, u32[]{:S(2)}, u32[]{:S(2)}) async-start(f32[2,1,65536]{2,1,0:T(1,128)} %reshape.157), calls=%async_computation.2 | async-start | bytes 1048576 | tf_op jit(solution)/shard_map/all_to_all | solution.py:63
  8.2 7.6 %copy-start.2 = (s32[2]{0:T(128)S(1)}, s32[2]{0:T(128)}, u32[]{:S(2)}) copy-start(s32[2]{0:T(128)} %param.7) | copy-start | bytes 28
  8.4 7.4 %copy-start.1 = (s32[1,8,64]{2,1,0:T(8,128)S(1)}, s32[1,8,64]{2,1,0:T(8,128)}, u32[]{:S(2)}) copy-start(s32[1,8,64]{2,1,0:T(8,128)} %param.6) | copy-start | bytes 6148
  8.4 33.7 %all-to-all-start = ((f32[2,1,1,32,8,2,2,128]{7,6,3,5,0,2,1,4:T(2,128)}), f32[2,1,1,32,8,2,2,128]{7,6,3,5,0,2,1,4:T(2,128)S(1)}, u32[]{:S(2)}, u32[]{:S(2)}) async-start(f32[2,1,1,32,8,2,2,128]{7,6,3,5,0,2,1,4:T(2,128)} %copy.24), calls=%async_computation | async-start | bytes 2097152 | tf_op jit(solution)/shard_map/all_to_all | solution.py:56
where the time goes:
time: 92.9 us; the launch traced here: 92.5 us
  blocking collectives  36.2 us (39%)
  waiting for transfers between devices  19.1 us (21%)
  local copies, waits for them, and re-layouts  12.7 us (14%)
  starting transfers between devices  10.9 us (12%)
  matrix products  8.13 us (9%)
  other arithmetic  4.67 us (5%)
    psum x1, blocking collectives, body(): total = lax.psum(jnp.sum(energies, axis=0), ('range', 'sub'))  31.6 us
    all_to_all x1, waiting for transfers between devices, body(): lax.all_to_all(spread, 'range', split_axis=4, concat_axis=1, tiled=True)  18.9 us
    all_to_all x1, starting transfers between devices, body(): lax.all_to_all(spread, 'range', split_axis=4, concat_axis=1, tiled=True)  7.41 us
    all_to_all x1, blocking collectives, body(): lax.all_to_all(lax.all_to_all(spread, 'range', split_axis=4, concat_axis=...  4.58 us
    all_to_all x3, local copies, waits for them, and re-layouts, body(): lax.all_to_all(beam_weights, 'sub', split_axis=0, concat_axis=4, tiled=True)  4.18 us
    all_to_all x1, starting transfers between devices, body(): lax.all_to_all(beam_weights, 'sub', split_axis=0, concat_axis=4, tiled=True)  3.49 us
    unnamed x8, local copies, waits for them, and re-layouts  3.15 us
    gather x4, local copies, waits for them, and re-layouts, block_terms(): picked = jnp.take(snaps, chosen, axis=1)  2.5 us
  transfers between devices with their start and end apart: 2, of which 2 were waited for; matrix products, arithmetic and copies ran while one was open for 8% of the time, Pallas kernels for 0%

commit v1 on v0

--- a/solution.py
+++ b/solution.py
@@ -70,7 +70,9 @@
     beams = filts.shape[2]
     filtered = filts.reshape(blocks_dev, parts_iq, beams, GB, pulses).transpose(1, 2, 0, 3, 4)
     filtered = filtered.reshape(parts_iq, beams, gate_dev, pulses)
-    total = lax.psum(jnp.sum(energies, axis=0), ("range", "sub"))
+    part = jnp.sum(energies, axis=0)
+    blocks = lax.all_gather(part, ("range", "sub"))
+    total = jnp.sum(blocks, axis=0)
     energy = total / (all_gates * pulses)
     return (covs, filtered, energy)
 

time: 92.9 us -> 80.7 us (0.87)
  blocking collectives: 36.2 us -> 24 us
    psum x1 -> x0, blocking collectives: 31.6 us -> none  [body(): total = lax.psum(jnp.sum(energies, axis=0), ('range', 'sub'))]
    all_gather x0 -> x1, blocking collectives: none -> 19.5 us  [body(): blocks = lax.all_gather(part, ('range', 'sub'))]
  transfers between devices with their start and end apart: 2 -> 2, of which waited for: 2 -> 2; matrix products, arithmetic and copies ran while one was open for 8% -> 9% of each run, Pallas kernels for 0% -> 0%
where the time goes in v1:
time: 80.7 us; the launch traced here: 80.3 us
  blocking collectives  24 us (30%)
  waiting for transfers between devices  19.1 us (24%)
  local copies, waits for them, and re-layouts  12.7 us (16%)
  starting transfers between devices  10.9 us (14%)
  matrix products  8.13 us (10%)
  other arithmetic  4.7 us (6%)
  between operations  0.84 us (1%)
    all_gather x1, blocking collectives, body(): blocks = lax.all_gather(part, ('range', 'sub'))  19.5 us
    all_to_all x1, waiting for transfers between devices, body(): lax.all_to_all(spread, 'range', split_axis=4, concat_axis=1, tiled=True)  18.9 us
    all_to_all x1, starting transfers between devices, body(): lax.all_to_all(spread, 'range', split_axis=4, concat_axis=1, tiled=True)  7.41 us
    all_to_all x1, blocking collectives, body(): lax.all_to_all(lax.all_to_all(spread, 'range', split_axis=4, concat_axis=...  4.58 us
    all_to_all x3, local copies, waits for them, and re-layouts, body(): lax.all_to_all(beam_weights, 'sub', split_axis=0, concat_axis=4, tiled=True)  4.18 us
    all_to_all x1, starting transfers between devices, body(): lax.all_to_all(beam_weights, 'sub', split_axis=0, concat_axis=4, tiled=True)  3.49 us
    unnamed x8, local copies, waits for them, and re-layouts  3.15 us
    gather x4, local copies, waits for them, and re-layouts, block_terms(): picked = jnp.take(snaps, chosen, axis=1)  2.5 us
  transfers between devices with their start and end apart: 2, of which 2 were waited for; matrix products, arithmetic and copies ran while one was open for 9% of the time, Pallas kernels for 0%

profile of v1, /device:TPU:0, one launch (start us, length us, event | category | flops | bytes accessed | tf_op | source)
XLA Modules:
  0.0 80.3 jit_solution(303801115158308347)
XLA Ops:
  0.6 2.5 %reshape.161 = f32[2,1,65536]{2,1,0:T(1,128)} reshape(f32[2,8,2,64,64]{4,3,2,1,0:T(8,128)} %param.5) | data formatting | bytes 1048576
  3.2 3.5 %all-to-all-start.2 = ((f32[2,1,65536]{2,1,0:T(1,128)}), f32[2,1,65536]{2,1,0:T(1,128)S(1)}, u32[]{:S(2)}, u32[]{:S(2)}) async-start(f32[2,1,65536]{2,1,0:T(1,128)} %reshape.161), calls=%async_computation.2 | async-start | bytes 1048576 | tf_op jit(solution)/shard_map/all_to_all | solution.py:63
  6.7 1.6 %copy.24 = f32[2,1,1,32,8,2,2,128]{7,6,3,5,0,2,1,4:T(2,128)} copy(f32[2,1,1,32,8,2,2,128]{7,6,5,4,3,0,2,1:T(2,128)S(1)} %bitcast.104) | data formatting | bytes 2097152 | tf_op jit(solution)/shard_map/reshape | solution.py:54
  8.2 0.2 all-to-all-done.2
  8.4 7.4 %all-to-all-start = ((f32[2,1,1,32,8,2,2,128]{7,6,3,5,0,2,1,4:T(2,128)}), f32[2,1,1,32,8,2,2,128]{7,6,3,5,0,2,1,4:T(2,128)S(1)}, u32[]{:S(2)}, u32[]{:S(2)}) async-start(f32[2,1,1,32,8,2,2,128]{7,6,3,5,0,2,1,4:T(2,128)} %copy.24), calls=%async_computation | async-start | bytes 2097152 | tf_op jit(solution)/shard_map/all_to_all | solution.py:56
  15.9 0.5 broadcast.75
  16.4 2.3 %reduce.6 = f32[2,65536]{1,0:T(2,128)S(1)} reduce(f32[2,1,65536]{2,1,0:T(1,128)S(1)} %all-to-all-done.2, f32[]{:T(128)} %broadcast.75), dimensions={1}, to_apply=%all_to_all.44.reduce_sub_computation | reduce | bytes 1048580 | tf_op jit(solution)/shard_map/all_to_all | solution.py:63
  18.8 0.6 reshape.162
  19.4 1.9 %copy.29 = f32[1,8,2,64,2,64]{5,4,3,1,2,0:T(2,128)} copy(f32[1,8,2,64,2,64]{5,3,2,1,4,0:T(8,128)S(1)} %bitcast.99) | data formatting | bytes 1048576 | tf_op jit(solution)/shard_map/all_to_all | solution.py:63
  21.2 1.8 %all_to_all.47 = f32[1,8,2,64,128]{4,3,1,2,0:T(8,128)S(1)} reshape(f32[1,8,2,64,2,64]{5,4,3,1,2,0:T(2,128)} %copy.29) | data formatting | bytes 1048576 | tf_op jit(solution)/shard_map/all_to_all | solution.py:63
  23.1 18.9 %all-to-all-done = f32[2,1,1,32,8,2,2,128]{7,6,3,5,0,2,1,4:T(2,128)S(1)} async-done(((f32[2,1,1,32,8,2,2,128]{7,6,3,5,0,2,1,4:T(2,128)}), f32[2,1,1,32,8,2,2,128]{7,6,3,5,0,2,1,4:T(2,128)S(1)}, u32[]{:S(2)}, u32[]{:S(2)}) %all-to-all-start) | async-done | bytes 1048608 | tf_op jit(solution)/shard_map/all_to_all | solution.py:56
  42.1 4.6 %all_to_all.51 = f32[2,8,1,32,1,2,2,128]{7,6,3,1,0,4,2,5:T(2,128)S(1)} all-to-all(f32[2,8,1,32,1,2,2,128]{7,6,3,1,0,4,2,5:T(2,128)S(1)} %copy.25), channel_id=1, replica_groups=mesh['groups'=2,'range'=8,'sub'=2] {'sub'}, dimensions={5} | all-to-all | bytes 2097152 | tf_op jit(solution)/shard_map/all_to_all | solution.py:55
  46.8 0.8 %copy.27 = f32[1,2,512,256]{3,1,2,0:T(2,128)S(1)} copy(f32[1,2,512,256]{3,0,2,1:T(1,128)S(1)} %bitcast.101) | data formatting | bytes 2097152 | tf_op jit(solution)/shard_map/transpose;reshape | solution.py:62
  47.6 2.3 %gather_fusion = f32[512,2,256]{2,1,0:T(2,128)S(1)} fusion(f32[1,2,512,256]{3,1,2,0:T(2,128)S(1)} %copy.27, s32[512]{0:T(512)S(1)} %reshape.147), kind=kCustom, calls=%fused_computation | custom fusion | bytes 2101248 | tf_op jit(solution)/shard_map/vmap(jit(_take))/gather | solution.py:12
  50.1 0.1 broadcast_select_fusion
  50.2 1.0 %convolution_bitcast_fusion.2 = f32[256,128]{1,0:T(8,128)S(1)} fusion(f32[1,2,8,64,256]{4,3,2,1,0:T(8,128)S(1)} %broadcast_select_fusion, f32[1,8,2,64,128]{4,3,1,2,0:T(8,128)S(1)} %all_to_all.47), kind=kOutput, calls=%fused_computation.13 | convolution fusion | flops 201326592 | bytes 917504 | tf_op jit(solution)/shard_map/vmap(snk,snx->kx)/dot_general | solution.py:27
  51.2 1.0 %convolution_bitcast_fusion = f32[256,128]{1,0:T(8,128)S(1)} fusion(f32[1,2,8,64,256]{4,3,2,1,0:T(8,128)S(1)} %broadcast_select_fusion, f32[1,8,2,64,128]{4,3,1,2,0:T(8,128)S(1)} %all_to_all.47), kind=kOutput, calls=%fused_computation.11 | convolution fusion | flops 201326592 | bytes 917504 | tf_op jit(solution)/shard_map/vmap(snk,snx->kx)/dot_general | solution.py:30
  52.2 0.6 fusion.12
  52.9 0.6 fusion.2
  53.5 0.4 fusion.19
  53.9 0.4 fusion.18
  54.3 0.6 fusion.8
  54.9 1.0 %fusion.6 = f32[256,128]{1,0:T(8,128)S(1)} fusion(f32[256,128]{1,0:T(8,128)S(1)} %convolution_bitcast_fusion.2, f32[1,2,8,64,256]{4,3,2,1,0:T(8,128)S(1)} %broadcast_select_fusion, f32[1,8,2,64,128]{4,3,1,2,0:T(8,128)S(1)} %all_to_all.47), kind=kOutput, calls=%fused_computation.15 | convolution fusion | flops 201359360 | bytes 1048576 | tf_op jit(solution)/shard_map/vmap(snk,snx->kx)/dot_general | solution.py:27
  55.9 0.6 fusion.3
  56.5 0.4 fusion
  56.9 0.4 fusion.5
  57.4 1.0 %add_reduce_fusion = (f32[128]{0:T(128)S(1)}, f32[256,128]{1,0:T(8,128)S(1)}, f32[256,128]{1,0:T(8,128)S(1)}) fusion(f32[256,128]{1,0:T(8,128)S(1)} %fusion.6, f32[128]{0:T(128)S(1)} %add_rsqrt_fusion, f32[256,128]{1,0:T(8,128)S(1)} %convolution_bitcast_fusion, f32[1,8,2,64,128]{4,3,1,2,0:T(8,128)S(1)} %all_to_all.47, ...), kind=kOutput, calls=%fused_computation.36 | convolution fusion | flops 201555840 | bytes 1311744 | tf_op jit(solution)/shard_map/vmap(snk,snx->kx)/dot_general | solution.py:30
  58.4 0.1 copy.30
  58.5 19.5 %all-gather.1 = f32[16,1,128]{2,1,0:T(1,128)S(1)} all-gather(f32[1,1,128]{2,1,0:T(1,128)S(1)} %bitcast.107), channel_id=2, replica_groups=mesh['groups'=2,'range'=8,'sub'=2] {'range','sub'}, dimensions={0}, use_global_device_ids=true | all-gather | bytes 8704 | tf_op jit(solution)/shard_map/all_gather | solution.py:74
  78.0 0.5 broadcast_multiply_fusion.2
  78.7 0.8 %pad_maximum_fusion = f32[1,8,64,128]{3,2,1,0:T(8,128)} fusion(f32[1,8,64,64]{3,2,1,0:T(8,128)S(1)} %bitcast.103, f32[1,8,64,64]{3,2,1,0:T(8,128)S(1)} %bitcast.97), kind=kLoop, calls=%fused_computation.28 | loop fusion | flops 65536 | bytes 524288 | tf_op jit(solution)/shard_map/vmap()/concatenate | solution.py:43
  79.5 0.8 %pad_maximum_fusion.1 = f32[2,128,2,128]{3,2,1,0:T(2,128)} fusion(f32[1,128,2,128]{3,2,1,0:T(2,128)S(1)} %copy.31, f32[1,128,2,128]{3,2,1,0:T(2,128)S(1)} %copy.30), kind=kLoop, calls=%fused_computation.29 | loop fusion | flops 65536 | bytes 524288 | tf_op jit(solution)/shard_map/vmap()/stack | solution.py:41
  (19 shorter events, 0.6 us)
Async XLA Ops:
  0.6 6.0 %copy-start = (f32[2,32,32,128]{3,2,1,0:T(8,128)S(1)}, f32[2,32,32,128]{3,2,1,0:T(8,128)}, u32[]{:S(2)}) copy-start(f32[2,32,32,128]{3,2,1,0:T(8,128)} %param.4) | copy-start | bytes 3145732
  3.2 5.2 %all-to-all-start.2 = ((f32[2,1,65536]{2,1,0:T(1,128)}), f32[2,1,65536]{2,1,0:T(1,128)S(1)}, u32[]{:S(2)}, u32[]{:S(2)}) async-start(f32[2,1,65536]{2,1,0:T(1,128)} %reshape.161), calls=%async_computation.2 | async-start | bytes 1048576 | tf_op jit(solution)/shard_map/all_to_all | solution.py:63
  8.2 7.6 %copy-start.2 = (s32[2]{0:T(128)S(1)}, s32[2]{0:T(128)}, u32[]{:S(2)}) copy-start(s32[2]{0:T(128)} %param.7) | copy-start | bytes 28
  8.4 7.4 %copy-start.1 = (s32[1,8,64]{2,1,0:T(8,128)S(1)}, s32[1,8,64]{2,1,0:T(8,128)}, u32[]{:S(2)}) copy-start(s32[1,8,64]{2,1,0:T(8,128)} %param.6) | copy-start | bytes 6148
  8.4 33.7 %all-to-all-start = ((f32[2,1,1,32,8,2,2,128]{7,6,3,5,0,2,1,4:T(2,128)}), f32[2,1,1,32,8,2,2,128]{7,6,3,5,0,2,1,4:T(2,128)S(1)}, u32[]{:S(2)}, u32[]{:S(2)}) async-start(f32[2,1,1,32,8,2,2,128]{7,6,3,5,0,2,1,4:T(2,128)} %copy.24), calls=%async_computation | async-start | bytes 2097152 | tf_op jit(solution)/shard_map/all_to_all | solution.py:56
